TPU v7x, 256 devices: a whole 4x4x8 slice. The times are simulated.
256 devices in a mesh: gx: 16 (over z, core), gy: 16 (over x, y).
Axes of the slice: x: 4, y: 4, z: 8, core: 2. Of those that a mesh axis runs over, the one named last changes fastest.
Arguments:
- density: float32 [256, 256, 128], P('gx', 'gy'), may hold values from 0.05 to 40, as said below
Outputs:
- potential: float32 [256, 256, 128], P('gx', 'gy')
Inputs may be any that keep to these rules, and one draw needn't show every extreme that they name: `density`: densities are positive.
All inputs are finite; a program needn't handle non-finite values.
Results may differ from a plain program's by a relative error of at most 0.00014.
Values sent between devices are 32-bit elements; how exact they have to be, the bound alone decides.
A program may use at most 64 MiB of HBM per device.

v0:
```python
import jax
import jax.numpy as jnp
from jax import lax
from jax.sharding import Mesh
from jax.sharding import PartitionSpec as P

LEVELS = 4
NEWTON = 3
GX_GY = ("gx_0", "gx_1", "gy_0", "gy_1")
GX = ("gx_0", "gx_1")
GY = ("gy_0", "gy_1")
COUPLING = 0.1
FLOOR = 3.0


def extended(x, sides, width):
    for axis, dim in sides:
        peers, length = (lax.axis_size(axis), x.shape[dim])
        up = [(i, (i + 1) % peers) for i in range(peers)]
        down = [(j, i) for i, j in up]
        last = lax.slice_in_dim(x, length - width, length, axis=dim)
        leading = lax.slice_in_dim(x, 0, width, axis=dim)
        before = lax.ppermute(last, axis, up)
        after = lax.ppermute(leading, axis, down)
        x = jnp.concatenate([before, x, after], axis=dim)
    return x


def one_axis_at_a_time(x, axes):
    for axis in axes:
        x = lax.psum(x, axis)
    return x


def shifted(padded, off_x, off_y, off_z):
    size_x = padded.shape[0] - 2
    size_y = padded.shape[1] - 2
    size_z = padded.shape[2] - 2
    return padded[
        1 + off_x : 1 + off_x + size_x,
        1 + off_y : 1 + off_y + size_y,
        1 + off_z : 1 + off_z + size_z,
    ]


def hessian(padded, spacing_inv):
    center = shifted(padded, 0, 0, 0)
    pure_x = (shifted(padded, 1, 0, 0) + shifted(padded, -1, 0, 0) - 2.0 * center) * spacing_inv
    pure_y = (shifted(padded, 0, 1, 0) + shifted(padded, 0, -1, 0) - 2.0 * center) * spacing_inv
    pure_z = (shifted(padded, 0, 0, 1) + shifted(padded, 0, 0, -1) - 2.0 * center) * spacing_inv
    quarter = 0.25 * spacing_inv
    mixed_xy = (
        shifted(padded, 1, 1, 0)
        - shifted(padded, 1, -1, 0)
        - shifted(padded, -1, 1, 0)
        + shifted(padded, -1, -1, 0)
    ) * quarter
    mixed_xz = (
        shifted(padded, 1, 0, 1)
        - shifted(padded, 1, 0, -1)
        - shifted(padded, -1, 0, 1)
        + shifted(padded, -1, 0, -1)
    ) * quarter
    mixed_yz = (
        shifted(padded, 0, 1, 1)
        - shifted(padded, 0, 1, -1)
        - shifted(padded, 0, -1, 1)
        + shifted(padded, 0, -1, -1)
    ) * quarter
    return (pure_x, pure_y, pure_z, mixed_xy, mixed_xz, mixed_yz)


def nonlinear(padded, source):
    pure_x, pure_y, pure_z, mixed_xy, mixed_xz, mixed_yz = hessian(padded, 1.0)
    cubic = 2.0 * (
        pure_x * pure_y
        + pure_x * pure_z
        + pure_y * pure_z
        - mixed_xy * mixed_xy
        - mixed_xz * mixed_xz
        - mixed_yz * mixed_yz
    )
    return pure_x + pure_y + pure_z + COUPLING * cubic - source


def coefficients(padded, spacing_inv):
    pure_x, pure_y, pure_z, mixed_xy, mixed_xz, mixed_yz = hessian(padded, spacing_inv)
    stiff_x = 1.0 + 2.0 * COUPLING * (pure_y + pure_z)
    stiff_y = 1.0 + 2.0 * COUPLING * (pure_x + pure_z)
    stiff_z = 1.0 + 2.0 * COUPLING * (pure_x + pure_y)
    diagonal = jnp.maximum(2.0 * (stiff_x + stiff_y + stiff_z), FLOOR)
    relax = 1.0 / (spacing_inv * diagonal)
    return jnp.stack(
        [
            stiff_x,
            stiff_y,
            stiff_z,
            -4.0 * COUPLING * mixed_xy,
            -4.0 * COUPLING * mixed_xz,
            -4.0 * COUPLING * mixed_yz,
            relax,
        ]
    )


def jacobian(padded, weights, spacing_inv):
    parts = hessian(padded, spacing_inv)
    result = weights[0] * parts[0]
    for index in range(1, 6):
        result = result + weights[index] * parts[index]
    return result


def restrict(field):
    size_x, size_y, size_z = field.shape
    blocks = field.reshape(size_x // 2, 2, size_y // 2, 2, size_z // 2, 2)
    return jnp.sum(blocks, axis=(1, 3, 5)) * 0.125


def prolong(field):
    size_x, size_y, size_z = field.shape
    spread = jnp.broadcast_to(field[:, None, :, None, :, None], (size_x, 2, size_y, 2, size_z, 2))
    return spread.reshape(2 * size_x, 2 * size_y, 2 * size_z)


def wrap_depth(field):
    return jnp.concatenate([field[..., -1:], field, field[..., :1]], axis=-1)


def extend(field):
    return wrap_depth(extended(field, ((GX, 0), (GY, 1)), 1))


def checker(shape, first_x, first_y, first_z):
    index_x = first_x + jnp.arange(shape[0], dtype=jnp.int32)
    index_y = first_y + jnp.arange(shape[1], dtype=jnp.int32)
    index_z = first_z + jnp.arange(shape[2], dtype=jnp.int32)
    parity = (index_x[:, None, None] + index_y[None, :, None] + index_z[None, None, :]) % 2
    return (parity == 0).astype(jnp.float32)


def black_half(change, target, weights, red_mask, pad_field, spacing_inv):
    black_mask = 1.0 - red_mask
    return (
        change
        + black_mask * (jacobian(pad_field(change), weights, spacing_inv) - target) * weights[6]
    )


def first_sweep(target, weights, red_mask, pad_field, spacing_inv):
    change = -red_mask * target * weights[6]
    return black_half(change, target, weights, red_mask, pad_field, spacing_inv)


def full_sweep(change, target, weights, red_mask, pad_field, spacing_inv):
    change = (
        change
        + red_mask * (jacobian(pad_field(change), weights, spacing_inv) - target) * weights[6]
    )
    return black_half(change, target, weights, red_mask, pad_field, spacing_inv)


def edge_terms():
    return None


def start_sweep(target, context):
    weights, red_mask, spacing_inv, wide = context
    return first_sweep(target, weights, red_mask, extend, spacing_inv)


def more_sweep(change, target, context):
    weights, red_mask, spacing_inv, wide = context
    return full_sweep(change, target, weights, red_mask, extend, spacing_inv)


def cycle(coarse_level, target, weight_levels, mask_levels, wide_masks):
    spacing_inv = 0.25**coarse_level
    weights = weight_levels[coarse_level]
    red_mask = mask_levels[coarse_level]
    context = (weights, red_mask, spacing_inv, edge_terms())
    change = start_sweep(target, context)
    if coarse_level == LEVELS - 1:
        change = more_sweep(change, target, context)
        return change
    leftover = target - jacobian(extend(change), weights, spacing_inv)
    change = change + prolong(
        cycle(coarse_level + 1, restrict(leftover), weight_levels, mask_levels, wide_masks)
    )
    return more_sweep(change, target, context)


def per_device(density):
    cells_total = float(density.size * lax.axis_size(GX) * lax.axis_size(GY))
    mass_total = one_axis_at_a_time(jnp.sum(density), GX_GY)
    source = density / (mass_total / cells_total) - 1.0
    mask_levels = []
    wide_masks = []
    for coarse_level in range(LEVELS):
        shape = (
            density.shape[0] >> coarse_level,
            density.shape[1] >> coarse_level,
            density.shape[2] >> coarse_level,
        )
        start_x = lax.axis_index(GX) * shape[0]
        start_y = lax.axis_index(GY) * shape[1]
        mask_levels.append(checker(shape, start_x, start_y, 0))
        wide_shape = (shape[0] + 2, shape[1] + 2, shape[2] + 2)
        wide_masks.append(checker(wide_shape, start_x - 1, start_y - 1, -1))

    def newton_turn(newton_step, potential):
        padded_levels = []
        coarse = potential
        for coarse_level in range(LEVELS):
            if coarse_level > 0:
                coarse = restrict(coarse)
            padded_levels.append(extend(coarse))
        weight_levels = [
            coefficients(padded_levels[coarse_level], 0.25**coarse_level)
            for coarse_level in range(LEVELS)
        ]
        target = -nonlinear(padded_levels[0], source)
        return potential + cycle(0, target, weight_levels, mask_levels, wide_masks)

    return lax.fori_loop(0, NEWTON, newton_turn, jnp.zeros_like(density))


def solution(mesh):
    torus = Mesh(mesh.devices.reshape(8, 2, 4, 4), ("gx_0", "gx_1", "gy_0", "gy_1"))
    placed = (P(GX, GY, None),)
    return jax.shard_map(
        per_device, mesh=torus, in_specs=placed, out_specs=P(GX, GY, None), check_vma=False
    )
```

profile of v0, /device:TPU:0, one launch (start us, length us, event | category | flops | bytes accessed | tf_op | source)
XLA Modules:
  0.0 816.9 jit_solution(15661478614758730707)
XLA Ops:
  1.6 19.0 %psum.28 = f32[]{:T(128)} all-reduce(f32[]{:T(128)} %reduce_sum.87), channel_id=1, replica_groups=mesh['gx_0'=8,'gx_1'=2,'gy_0'=4,'gy_1'=4] {'gx_0'}, use_global_device_ids=true, to_apply=%region_1.0 | all-reduce | flops 1 | bytes 8 | tf_op jit(solution)/shard_map/psum | solution.py:31
  23.7 11.2 %psum.30 = f32[]{:T(128)} all-reduce(f32[]{:T(128)} %psum.29), channel_id=1, replica_groups=mesh['gx_0'=8,'gx_1'=2,'gy_0'=4,'gy_1'=4] {'gy_0'}, use_global_device_ids=true, to_apply=%region_3.0 | all-reduce | flops 1 | bytes 8 | tf_op jit(solution)/shard_map/psum | solution.py:31
  34.9 11.4 %psum.31 = f32[]{:T(128)} all-reduce(f32[]{:T(128)} %psum.30), channel_id=1, replica_groups=mesh['gx_0'=8,'gx_1'=2,'gy_0'=4,'gy_1'=4] {'gy_1'}, use_global_device_ids=true, to_apply=%region_4.0 | all-reduce | flops 1 | bytes 8 | tf_op jit(solution)/shard_map/psum | solution.py:31
  48.2 767.6 %while.16 = (s32[]{:T(128)}, f32[16,16,128]{2,1,0:T(8,128)S(1)}, f32[16,16,128]{2,1,0:T(8,128)S(1)}, s32[16,16]{1,0:T(8,128)S(1)}, s32[8,8]{1,0:T(8,128)S(1)}, /...) while((s32[]{:T(128)}, f32[16,16,128]{2,1,0:T(8,128)S(1)}, ...), condition=%wide.region_12.13_spmd.clone.clone.clone, body=%wide.region_5.12_spmd.clone.clone.clone.sunk | while | flops 16104283 | bytes 31824424 | solution.py:225
  49.2 9.8 %reshape.257 = f32[8,2,8,2,64,2]{5,4,3,2,1,0:T(8,128)} reshape(f32[16,16,128]{2,1,0:T(8,128)S(1)} %broadcast_select_fusion.2) | data formatting | bytes 262144 | tf_op jit(solution)/shard_map/while/body/eval_jaxpr/reshape | solution.py:116
  59.0 4.0 reduce_sum.113
  75.5 5.4 collective-permute-start.39
  89.5 5.7 collective-permute-done.15
  95.2 4.2 collective-permute-done.5
  103.2 3.4 collective-permute-done.7
  120.0 9.8 %reshape.256 = f32[8,2,8,2,64,2]{5,4,3,2,1,0:T(8,128)} reshape(f32[16,16,128]{2,1,0:T(8,128)S(1)} %fusion.546) | data formatting | bytes 262144 | tf_op jit(solution)/shard_map/while/body/eval_jaxpr/reshape | solution.py:116
  129.8 4.0 reduce_sum.112
  142.0 5.3 collective-permute-done.19
  155.7 3.4 collective-permute-done.23
  168.8 3.4 collective-permute-done.31
  180.5 3.6 collective-permute-done.35
  204.3 3.4 collective-permute-done.47
  239.5 3.4 collective-permute-done.59
  268.2 4.0 broadcast_in_dim.60
  272.2 6.9 reshape.262
  304.6 9.8 %reshape.257 = f32[8,2,8,2,64,2]{5,4,3,2,1,0:T(8,128)} reshape(f32[16,16,128]{2,1,0:T(8,128)S(1)} %broadcast_select_fusion.2) | data formatting | bytes 262144 | tf_op jit(solution)/shard_map/while/body/eval_jaxpr/reshape | solution.py:116
  314.4 4.0 reduce_sum.113
  330.9 5.4 collective-permute-start.39
  344.9 5.7 collective-permute-done.15
  350.6 4.2 collective-permute-done.5
  358.6 3.4 collective-permute-done.7
  375.6 9.8 %reshape.256 = f32[8,2,8,2,64,2]{5,4,3,2,1,0:T(8,128)} reshape(f32[16,16,128]{2,1,0:T(8,128)S(1)} %fusion.546) | data formatting | bytes 262144 | tf_op jit(solution)/shard_map/while/body/eval_jaxpr/reshape | solution.py:116
  385.4 4.0 reduce_sum.112
  397.6 5.3 collective-permute-done.19
  436.1 3.6 collective-permute-done.35
  448.3 3.4 collective-permute-done.43
  471.5 3.4 collective-permute-done.51
  483.4 3.4 collective-permute-done.55
  523.6 4.0 broadcast_in_dim.60
  527.5 6.9 reshape.262
  542.6 3.4 collective-permute-done.71
  554.9 3.4 collective-permute-done.75
  560.2 9.8 %reshape.257 = f32[8,2,8,2,64,2]{5,4,3,2,1,0:T(8,128)} reshape(f32[16,16,128]{2,1,0:T(8,128)S(1)} %broadcast_select_fusion.2) | data formatting | bytes 262144 | tf_op jit(solution)/shard_map/while/body/eval_jaxpr/reshape | solution.py:116
  570.0 4.0 reduce_sum.113
  586.5 5.4 collective-permute-start.39
  600.5 5.7 collective-permute-done.15
  606.2 4.2 collective-permute-done.5
  631.0 9.8 %reshape.256 = f32[8,2,8,2,64,2]{5,4,3,2,1,0:T(8,128)} reshape(f32[16,16,128]{2,1,0:T(8,128)S(1)} %fusion.546) | data formatting | bytes 262144 | tf_op jit(solution)/shard_map/while/body/eval_jaxpr/reshape | solution.py:116
  640.8 4.0 reduce_sum.112
  653.0 5.3 collective-permute-done.19
  691.5 3.6 collective-permute-done.35
  779.2 4.0 broadcast_in_dim.60
  783.1 6.9 reshape.262
  (906 shorter events, 543.4 us)
Async XLA Ops:
  48.7 26.8 %collective-permute-start = (f32[1,16,128]{2,1,0:T(8,128)S(1)}, f32[1,16,128]{2,1,0:T(8,128)S(1)}, u32[]{:S(2)}, u32[]{:S(2)}) collective-permute-start(f32[1,16,128]{2,1,0:T(8,128)S(1)} %get-tuple-element.774), channel_id=1, source_target_pairs={{16,0},{32,16},{48,32},{64,48},{80,64},{96,80},{112,96},{128,112},... | collective-permute-start | bytes 24584 | tf_op jit(solution)/shard_map/while/body/eval_jaxpr/ppermute | solution.py:24
  48.7 32.2 %collective-permute-start.1 = (f32[1,16,128]{2,1,0:T(8,128)S(1)}, f32[1,16,128]{2,1,0:T(8,128)S(1)}, u32[]{:S(2)}, u32[]{:S(2)}) collective-permute-start(f32[1,16,128]{2,1,0:T(8,128)S(1)} %get-tuple-element.775), channel_id=1, source_target_pairs={{0,16},{16,32},{32,48},{48,64},{64,80},{80,96},{96,112},{112,128},... | collective-permute-start | bytes 24584 | tf_op jit(solution)/shard_map/while/body/eval_jaxpr/ppermute | solution.py:23
  63.1 18.0 %collective-permute-start.12 = (f32[1,8,64]{2,1,0:T(8,128)S(1)}, f32[1,8,64]{2,1,0:T(8,128)S(1)}, u32[]{:S(2)}, u32[]{:S(2)}) collective-permute-start(f32[1,8,64]{2,1,0:T(8,128)S(1)} %get-tuple-element.814), channel_id=1, source_target_pairs={{16,0},{32,16},{48,32},{64,48},{80,64},{96,80},{112,96},{128,112},... | collective-permute-start | bytes 6152 | tf_op jit(solution)/shard_map/while/body/eval_jaxpr/ppermute | solution.py:24
  72.6 8.6 %collective-permute-start.13 = (f32[1,8,64]{2,1,0:T(8,128)S(1)}, f32[1,8,64]{2,1,0:T(8,128)S(1)}, u32[]{:S(2)}, u32[]{:S(2)}) collective-permute-start(f32[1,8,64]{2,1,0:T(8,128)S(1)} %get-tuple-element.815), channel_id=1, source_target_pairs={{0,16},{16,32},{32,48},{48,64},{64,80},{80,96},{96,112},{112,128},... | collective-permute-start | bytes 6152 | tf_op jit(solution)/shard_map/while/body/eval_jaxpr/ppermute | solution.py:23
  75.5 85.9 %collective-permute-start.38 = (f32[4,1,16]{2,1,0:T(1,128)S(1)}, f32[4,1,16]{2,1,0:T(1,128)S(1)}, u32[]{:S(2)}, u32[]{:S(2)}) collective-permute-start(f32[4,1,16]{2,1,0:T(1,128)S(1)} %get-tuple-element.892), channel_id=1, source_target_pairs={{0,1},{1,2},{2,3},{3,4},{4,5},{5,6},{6,7},{7,8},{8,9},{9,10},{10,1... | collective-permute-start | bytes 776 | tf_op jit(solution)/shard_map/while/body/eval_jaxpr/ppermute | solution.py:23
  75.5 85.9 %collective-permute-start.39 = (f32[4,1,16]{2,1,0:T(1,128)S(1)}, f32[4,1,16]{2,1,0:T(1,128)S(1)}, u32[]{:S(2)}, u32[]{:S(2)}) collective-permute-start(f32[4,1,16]{2,1,0:T(1,128)S(1)} %get-tuple-element.893), channel_id=1, source_target_pairs={{1,0},{2,1},{3,2},{4,3},{5,4},{6,5},{7,6},{8,7},{9,8},{10,9},{11,1... | collective-permute-start | bytes 776 | tf_op jit(solution)/shard_map/while/body/eval_jaxpr/ppermute | solution.py:24
  81.0 53.0 %collective-permute-start.26 = (f32[6,1,32]{2,1,0:T(1,128)S(1)}, f32[6,1,32]{2,1,0:T(1,128)S(1)}, u32[]{:S(2)}, u32[]{:S(2)}) collective-permute-start(f32[6,1,32]{2,1,0:T(1,128)S(1)} %get-tuple-element.854), channel_id=1, source_target_pairs={{1,0},{2,1},{3,2},{4,3},{5,4},{6,5},{7,6},{8,7},{9,8},{10,9},{11,1... | collective-permute-start | bytes 2312 | tf_op jit(solution)/shard_map/while/body/eval_jaxpr/ppermute | solution.py:24
  81.2 7.1 collective-permute-start.3
  99.6 7.1 collective-permute-start.7
  112.1 7.1 collective-permute-start.11
  115.8 18.7 %collective-permute-start.27 = (f32[6,1,32]{2,1,0:T(1,128)S(1)}, f32[6,1,32]{2,1,0:T(1,128)S(1)}, u32[]{:S(2)}, u32[]{:S(2)}) collective-permute-start(f32[6,1,32]{2,1,0:T(1,128)S(1)} %get-tuple-element.855), channel_id=1, source_target_pairs={{0,1},{1,2},{2,3},{3,4},{4,5},{5,6},{6,7},{7,8},{8,9},{9,10},{10,1... | collective-permute-start | bytes 2312 | tf_op jit(solution)/shard_map/while/body/eval_jaxpr/ppermute | solution.py:23
  152.1 7.0 collective-permute-start.23
  176.9 7.2 collective-permute-start.35
  248.5 7.0 collective-permute-start.63
  260.7 7.0 collective-permute-start.67
  283.5 7.1 collective-permute-start.71
  295.9 7.1 collective-permute-start.75
  304.1 26.8 %collective-permute-start = (f32[1,16,128]{2,1,0:T(8,128)S(1)}, f32[1,16,128]{2,1,0:T(8,128)S(1)}, u32[]{:S(2)}, u32[]{:S(2)}) collective-permute-start(f32[1,16,128]{2,1,0:T(8,128)S(1)} %get-tuple-element.774), channel_id=1, source_target_pairs={{16,0},{32,16},{48,32},{64,48},{80,64},{96,80},{112,96},{128,112},... | collective-permute-start | bytes 24584 | tf_op jit(solution)/shard_map/while/body/eval_jaxpr/ppermute | solution.py:24
  304.1 32.2 %collective-permute-start.1 = (f32[1,16,128]{2,1,0:T(8,128)S(1)}, f32[1,16,128]{2,1,0:T(8,128)S(1)}, u32[]{:S(2)}, u32[]{:S(2)}) collective-permute-start(f32[1,16,128]{2,1,0:T(8,128)S(1)} %get-tuple-element.775), channel_id=1, source_target_pairs={{0,16},{16,32},{32,48},{48,64},{64,80},{80,96},{96,112},{112,128},... | collective-permute-start | bytes 24584 | tf_op jit(solution)/shard_map/while/body/eval_jaxpr/ppermute | solution.py:23
  318.4 18.0 %collective-permute-start.12 = (f32[1,8,64]{2,1,0:T(8,128)S(1)}, f32[1,8,64]{2,1,0:T(8,128)S(1)}, u32[]{:S(2)}, u32[]{:S(2)}) collective-permute-start(f32[1,8,64]{2,1,0:T(8,128)S(1)} %get-tuple-element.814), channel_id=1, source_target_pairs={{16,0},{32,16},{48,32},{64,48},{80,64},{96,80},{112,96},{128,112},... | collective-permute-start | bytes 6152 | tf_op jit(solution)/shard_map/while/body/eval_jaxpr/ppermute | solution.py:24
  328.0 8.6 %collective-permute-start.13 = (f32[1,8,64]{2,1,0:T(8,128)S(1)}, f32[1,8,64]{2,1,0:T(8,128)S(1)}, u32[]{:S(2)}, u32[]{:S(2)}) collective-permute-start(f32[1,8,64]{2,1,0:T(8,128)S(1)} %get-tuple-element.815), channel_id=1, source_target_pairs={{0,16},{16,32},{32,48},{48,64},{64,80},{80,96},{96,112},{112,128},... | collective-permute-start | bytes 6152 | tf_op jit(solution)/shard_map/while/body/eval_jaxpr/ppermute | solution.py:23
  330.9 86.1 %collective-permute-start.38 = (f32[4,1,16]{2,1,0:T(1,128)S(1)}, f32[4,1,16]{2,1,0:T(1,128)S(1)}, u32[]{:S(2)}, u32[]{:S(2)}) collective-permute-start(f32[4,1,16]{2,1,0:T(1,128)S(1)} %get-tuple-element.892), channel_id=1, source_target_pairs={{0,1},{1,2},{2,3},{3,4},{4,5},{5,6},{6,7},{7,8},{8,9},{9,10},{10,1... | collective-permute-start | bytes 776 | tf_op jit(solution)/shard_map/while/body/eval_jaxpr/ppermute | solution.py:23
  330.9 86.1 %collective-permute-start.39 = (f32[4,1,16]{2,1,0:T(1,128)S(1)}, f32[4,1,16]{2,1,0:T(1,128)S(1)}, u32[]{:S(2)}, u32[]{:S(2)}) collective-permute-start(f32[4,1,16]{2,1,0:T(1,128)S(1)} %get-tuple-element.893), channel_id=1, source_target_pairs={{1,0},{2,1},{3,2},{4,3},{5,4},{6,5},{7,6},{8,7},{9,8},{10,9},{11,1... | collective-permute-start | bytes 776 | tf_op jit(solution)/shard_map/while/body/eval_jaxpr/ppermute | solution.py:24
  336.3 53.3 %collective-permute-start.26 = (f32[6,1,32]{2,1,0:T(1,128)S(1)}, f32[6,1,32]{2,1,0:T(1,128)S(1)}, u32[]{:S(2)}, u32[]{:S(2)}) collective-permute-start(f32[6,1,32]{2,1,0:T(1,128)S(1)} %get-tuple-element.854), channel_id=1, source_target_pairs={{1,0},{2,1},{3,2},{4,3},{5,4},{6,5},{7,6},{8,7},{9,8},{10,9},{11,1... | collective-permute-start | bytes 2312 | tf_op jit(solution)/shard_map/while/body/eval_jaxpr/ppermute | solution.py:24
  336.6 7.1 collective-permute-start.3
  355.0 7.1 collective-permute-start.7
  367.8 7.1 collective-permute-start.11
  371.4 18.7 %collective-permute-start.27 = (f32[6,1,32]{2,1,0:T(1,128)S(1)}, f32[6,1,32]{2,1,0:T(1,128)S(1)}, u32[]{:S(2)}, u32[]{:S(2)}) collective-permute-start(f32[6,1,32]{2,1,0:T(1,128)S(1)} %get-tuple-element.855), channel_id=1, source_target_pairs={{0,1},{1,2},{2,3},{3,4},{4,5},{5,6},{6,7},{7,8},{8,9},{9,10},{10,1... | collective-permute-start | bytes 2312 | tf_op jit(solution)/shard_map/while/body/eval_jaxpr/ppermute | solution.py:23
  407.7 7.0 collective-permute-start.23
  432.6 7.2 collective-permute-start.35
  504.1 7.0 collective-permute-start.63
  538.9 7.1 collective-permute-start.71
  551.3 7.1 collective-permute-start.75
  559.7 26.8 %collective-permute-start = (f32[1,16,128]{2,1,0:T(8,128)S(1)}, f32[1,16,128]{2,1,0:T(8,128)S(1)}, u32[]{:S(2)}, u32[]{:S(2)}) collective-permute-start(f32[1,16,128]{2,1,0:T(8,128)S(1)} %get-tuple-element.774), channel_id=1, source_target_pairs={{16,0},{32,16},{48,32},{64,48},{80,64},{96,80},{112,96},{128,112},... | collective-permute-start | bytes 24584 | tf_op jit(solution)/shard_map/while/body/eval_jaxpr/ppermute | solution.py:24
  559.7 32.2 %collective-permute-start.1 = (f32[1,16,128]{2,1,0:T(8,128)S(1)}, f32[1,16,128]{2,1,0:T(8,128)S(1)}, u32[]{:S(2)}, u32[]{:S(2)}) collective-permute-start(f32[1,16,128]{2,1,0:T(8,128)S(1)} %get-tuple-element.775), channel_id=1, source_target_pairs={{0,16},{16,32},{32,48},{48,64},{64,80},{80,96},{96,112},{112,128},... | collective-permute-start | bytes 24584 | tf_op jit(solution)/shard_map/while/body/eval_jaxpr/ppermute | solution.py:23
  574.1 18.0 %collective-permute-start.12 = (f32[1,8,64]{2,1,0:T(8,128)S(1)}, f32[1,8,64]{2,1,0:T(8,128)S(1)}, u32[]{:S(2)}, u32[]{:S(2)}) collective-permute-start(f32[1,8,64]{2,1,0:T(8,128)S(1)} %get-tuple-element.814), channel_id=1, source_target_pairs={{16,0},{32,16},{48,32},{64,48},{80,64},{96,80},{112,96},{128,112},... | collective-permute-start | bytes 6152 | tf_op jit(solution)/shard_map/while/body/eval_jaxpr/ppermute | solution.py:24
  583.6 8.6 %collective-permute-start.13 = (f32[1,8,64]{2,1,0:T(8,128)S(1)}, f32[1,8,64]{2,1,0:T(8,128)S(1)}, u32[]{:S(2)}, u32[]{:S(2)}) collective-permute-start(f32[1,8,64]{2,1,0:T(8,128)S(1)} %get-tuple-element.815), channel_id=1, source_target_pairs={{0,16},{16,32},{32,48},{48,64},{64,80},{80,96},{96,112},{112,128},... | collective-permute-start | bytes 6152 | tf_op jit(solution)/shard_map/while/body/eval_jaxpr/ppermute | solution.py:23
  586.5 85.9 %collective-permute-start.38 = (f32[4,1,16]{2,1,0:T(1,128)S(1)}, f32[4,1,16]{2,1,0:T(1,128)S(1)}, u32[]{:S(2)}, u32[]{:S(2)}) collective-permute-start(f32[4,1,16]{2,1,0:T(1,128)S(1)} %get-tuple-element.892), channel_id=1, source_target_pairs={{0,1},{1,2},{2,3},{3,4},{4,5},{5,6},{6,7},{7,8},{8,9},{9,10},{10,1... | collective-permute-start | bytes 776 | tf_op jit(solution)/shard_map/while/body/eval_jaxpr/ppermute | solution.py:23
  586.5 85.9 %collective-permute-start.39 = (f32[4,1,16]{2,1,0:T(1,128)S(1)}, f32[4,1,16]{2,1,0:T(1,128)S(1)}, u32[]{:S(2)}, u32[]{:S(2)}) collective-permute-start(f32[4,1,16]{2,1,0:T(1,128)S(1)} %get-tuple-element.893), channel_id=1, source_target_pairs={{1,0},{2,1},{3,2},{4,3},{5,4},{6,5},{7,6},{8,7},{9,8},{10,9},{11,1... | collective-permute-start | bytes 776 | tf_op jit(solution)/shard_map/while/body/eval_jaxpr/ppermute | solution.py:24
  591.9 53.0 %collective-permute-start.26 = (f32[6,1,32]{2,1,0:T(1,128)S(1)}, f32[6,1,32]{2,1,0:T(1,128)S(1)}, u32[]{:S(2)}, u32[]{:S(2)}) collective-permute-start(f32[6,1,32]{2,1,0:T(1,128)S(1)} %get-tuple-element.854), channel_id=1, source_target_pairs={{1,0},{2,1},{3,2},{4,3},{5,4},{6,5},{7,6},{8,7},{9,8},{10,9},{11,1... | collective-permute-start | bytes 2312 | tf_op jit(solution)/shard_map/while/body/eval_jaxpr/ppermute | solution.py:24
  592.2 7.1 collective-permute-start.3
  610.6 7.1 collective-permute-start.7
  623.1 7.1 collective-permute-start.11
  626.8 18.7 %collective-permute-start.27 = (f32[6,1,32]{2,1,0:T(1,128)S(1)}, f32[6,1,32]{2,1,0:T(1,128)S(1)}, u32[]{:S(2)}, u32[]{:S(2)}) collective-permute-start(f32[6,1,32]{2,1,0:T(1,128)S(1)} %get-tuple-element.855), channel_id=1, source_target_pairs={{0,1},{1,2},{2,3},{3,4},{4,5},{5,6},{6,7},{7,8},{8,9},{9,10},{10,1... | collective-permute-start | bytes 2312 | tf_op jit(solution)/shard_map/while/body/eval_jaxpr/ppermute | solution.py:23
  687.9 7.2 collective-permute-start.35
  771.7 7.0 collective-permute-start.67
  794.5 7.1 collective-permute-start.71
  806.9 7.1 collective-permute-start.75
  (181 other events, 689.4 us)
where the time goes:
time: 819 us; the launch traced here: 817 us
  waiting for transfers between devices  437 us (53%)
  starting transfers between devices  170 us (21%)
  local copies, waits for them, and re-layouts  107 us (13%)
  other arithmetic  51 us (6%)
  blocking collectives  44.7 us (5%)
    ppermute x114, waiting for transfers between devices, extended(): before = lax.ppermute(last, axis, up)  322 us
    ppermute x114, waiting for transfers between devices, extended(): after = lax.ppermute(leading, axis, down)  115 us
    ppermute x114, starting transfers between devices, extended(): before = lax.ppermute(last, axis, up)  115 us
    reshape x12, local copies, waits for them, and re-layouts, restrict(): blocks = field.reshape(size_x // 2, 2, size_y // 2, 2, size_z // 2, 2)  62.2 us
    ppermute x114, starting transfers between devices, extended(): after = lax.ppermute(leading, axis, down)  55.3 us
    psum x4, blocking collectives, one_axis_at_a_time(): x = lax.psum(x, axis)  44.7 us
    reduce_sum x18, other arithmetic, restrict(): return jnp.sum(blocks, axis=(1, 3, 5)) * 0.125  25.8 us
    reshape x9, local copies, waits for them, and re-layouts, prolong(): return spread.reshape(2 * size_x, 2 * size_y, 2 * size_z)  23 us
  transfers between devices with their start and end apart: 228, of which 198 were waited for; matrix products, arithmetic and copies ran while one was open for 13% of the time, Pallas kernels for 0%

commit v1 on v0

--- a/solution.py
+++ b/solution.py
@@ -28,7 +28,7 @@
 
 def one_axis_at_a_time(x, axes):
     for axis in axes:
-        x = lax.psum(x, axis)
+        x = jnp.sum(lax.all_gather(x, axis), axis=0)
     return x
 
 

time: 819 us -> 829 us (1.012)
  local copies, waits for them, and re-layouts: 107 us -> 118 us
    psum x4 -> x0, blocking collectives: 44.7 us -> none  [one_axis_at_a_time(): x = lax.psum(x, axis)]
    unnamed x0 -> x4, blocking collectives: none -> 41.9 us
    unnamed x2 -> x14, local copies, waits for them, and re-layouts: 0.65 us -> 11.4 us
where the time goes in v1:
time: 829 us; the launch traced here: 827 us
  waiting for transfers between devices  437 us (53%)
  starting transfers between devices  170 us (21%)
  local copies, waits for them, and re-layouts  118 us (14%)
  other arithmetic  53.5 us (6%)
  blocking collectives  41.9 us (5%)
    ppermute x114, waiting for transfers between devices, extended(): before = lax.ppermute(last, axis, up)  322 us
    ppermute x114, waiting for transfers between devices, extended(): after = lax.ppermute(leading, axis, down)  115 us
    ppermute x114, starting transfers between devices, extended(): before = lax.ppermute(last, axis, up)  115 us
    reshape x12, local copies, waits for them, and re-layouts, restrict(): blocks = field.reshape(size_x // 2, 2, size_y // 2, 2, size_z // 2, 2)  62 us
    ppermute x114, starting transfers between devices, extended(): after = lax.ppermute(leading, axis, down)  55.3 us
    unnamed x4, blocking collectives  41.9 us
    reduce_sum x18, other arithmetic, restrict(): return jnp.sum(blocks, axis=(1, 3, 5)) * 0.125  25.6 us
    reshape x9, local copies, waits for them, and re-layouts, prolong(): return spread.reshape(2 * size_x, 2 * size_y, 2 * size_z)  23 us
  transfers between devices with their start and end apart: 228, of which 198 were waited for; matrix products, arithmetic and copies ran while one was open for 13% of the time, Pallas kernels for 0%

profile of v1, /device:TPU:0, one launch (start us, length us, event | category | flops | bytes accessed | tf_op | source)
XLA Modules:
  0.0 827.0 jit_solution(2199285411326393953)
XLA Ops:
  8.3 18.3 %all-reduce = f32[8]{0:T(128)S(1)} all-reduce(f32[8]{0:T(128)S(1)} %dynamic-update-slice), channel_id=1, replica_groups=mesh['gx_0'=8,'gx_1'=2,'gy_0'=4,'gy_1'=4] {'gx_0'}, use_global_device_ids=true, to_apply=%add | all-reduce | flops 8 | bytes 64
  33.1 10.5 %all-reduce.2 = f32[4]{0:T(128)S(1)} all-reduce(f32[4]{0:T(128)S(1)} %dynamic-update-slice.2), channel_id=1, replica_groups=mesh['gx_0'=8,'gx_1'=2,'gy_0'=4,'gy_1'=4] {'gy_0'}, use_global_device_ids=true, to_apply=%add.2 | all-reduce | flops 4 | bytes 32
  45.7 10.7 %all-reduce.3 = f32[4]{0:T(128)S(1)} all-reduce(f32[4]{0:T(128)S(1)} %dynamic-update-slice.3), channel_id=1, replica_groups=mesh['gx_0'=8,'gx_1'=2,'gy_0'=4,'gy_1'=4] {'gy_1'}, use_global_device_ids=true, to_apply=%add.3 | all-reduce | flops 4 | bytes 32
  58.8 767.1 %while.16 = (s32[]{:T(128)}, f32[16,16,128]{2,1,0:T(8,128)S(1)}, f32[16,16,128]{2,1,0:T(8,128)S(1)}, s32[16,16]{1,0:T(8,128)S(1)}, s32[8,8]{1,0:T(8,128)S(1)}, /...) while((s32[]{:T(128)}, f32[16,16,128]{2,1,0:T(8,128)S(1)}, ...), condition=%wide.region_12.13_spmd.clone.clone.clone, body=%wide.region_5.12_spmd.clone.clone.clone.sunk | while | flops 16104283 | bytes 31824424 | solution.py:225
  59.8 9.7 %reshape.277 = f32[8,2,8,2,64,2]{5,4,3,2,1,0:T(8,128)} reshape(f32[16,16,128]{2,1,0:T(8,128)S(1)} %broadcast_select_fusion.2) | data formatting | bytes 262144 | tf_op jit(solution)/shard_map/while/body/eval_jaxpr/reshape | solution.py:116
  69.6 4.0 reduce_sum.153
  86.1 5.4 collective-permute-start.39
  100.0 5.7 collective-permute-done.15
  105.8 4.2 collective-permute-done.5
  130.5 9.8 %reshape.276 = f32[8,2,8,2,64,2]{5,4,3,2,1,0:T(8,128)} reshape(f32[16,16,128]{2,1,0:T(8,128)S(1)} %fusion.546) | data formatting | bytes 262144 | tf_op jit(solution)/shard_map/while/body/eval_jaxpr/reshape | solution.py:116
  140.3 4.0 reduce_sum.152
  152.4 5.3 collective-permute-done.19
  166.2 3.4 collective-permute-done.23
  191.0 3.6 collective-permute-done.35
  203.2 3.4 collective-permute-done.43
  238.3 3.4 collective-permute-done.55
  250.0 3.4 collective-permute-done.59
  278.6 4.0 broadcast_in_dim.60
  282.6 6.9 reshape.282
  297.6 3.4 collective-permute-done.71
  310.0 3.4 collective-permute-done.75
  315.0 9.7 %reshape.277 = f32[8,2,8,2,64,2]{5,4,3,2,1,0:T(8,128)} reshape(f32[16,16,128]{2,1,0:T(8,128)S(1)} %broadcast_select_fusion.2) | data formatting | bytes 262144 | tf_op jit(solution)/shard_map/while/body/eval_jaxpr/reshape | solution.py:116
  324.8 4.0 reduce_sum.153
  341.3 5.4 collective-permute-start.39
  355.2 5.7 collective-permute-done.15
  361.0 4.2 collective-permute-done.5
  386.0 9.8 %reshape.276 = f32[8,2,8,2,64,2]{5,4,3,2,1,0:T(8,128)} reshape(f32[16,16,128]{2,1,0:T(8,128)S(1)} %fusion.546) | data formatting | bytes 262144 | tf_op jit(solution)/shard_map/while/body/eval_jaxpr/reshape | solution.py:116
  395.7 4.0 reduce_sum.152
  407.9 5.3 collective-permute-done.19
  421.6 3.4 collective-permute-done.23
  434.7 3.4 collective-permute-done.31
  446.4 3.6 collective-permute-done.35
  470.2 3.4 collective-permute-done.47
  505.4 3.4 collective-permute-done.59
  530.0 3.4 collective-permute-done.67
  533.8 4.0 broadcast_in_dim.60
  537.8 6.9 reshape.282
  570.5 9.7 %reshape.277 = f32[8,2,8,2,64,2]{5,4,3,2,1,0:T(8,128)} reshape(f32[16,16,128]{2,1,0:T(8,128)S(1)} %broadcast_select_fusion.2) | data formatting | bytes 262144 | tf_op jit(solution)/shard_map/while/body/eval_jaxpr/reshape | solution.py:116
  580.2 4.0 reduce_sum.153
  596.7 5.4 collective-permute-start.39
  610.7 5.7 collective-permute-done.15
  616.4 4.2 collective-permute-done.5
  641.2 9.8 %reshape.276 = f32[8,2,8,2,64,2]{5,4,3,2,1,0:T(8,128)} reshape(f32[16,16,128]{2,1,0:T(8,128)S(1)} %fusion.546) | data formatting | bytes 262144 | tf_op jit(solution)/shard_map/while/body/eval_jaxpr/reshape | solution.py:116
  650.9 4.0 reduce_sum.152
  663.1 5.3 collective-permute-done.19
  701.6 3.6 collective-permute-done.35
  789.3 4.0 broadcast_in_dim.60
  793.2 6.9 reshape.282
  (922 shorter events, 556.1 us)
Async XLA Ops:
  59.3 26.8 %collective-permute-start = (f32[1,16,128]{2,1,0:T(8,128)S(1)}, f32[1,16,128]{2,1,0:T(8,128)S(1)}, u32[]{:S(2)}, u32[]{:S(2)}) collective-permute-start(f32[1,16,128]{2,1,0:T(8,128)S(1)} %get-tuple-element.774), channel_id=1, source_target_pairs={{16,0},{32,16},{48,32},{64,48},{80,64},{96,80},{112,96},{128,112},... | collective-permute-start | bytes 24584 | tf_op jit(solution)/shard_map/while/body/eval_jaxpr/ppermute | solution.py:24
  59.3 32.2 %collective-permute-start.1 = (f32[1,16,128]{2,1,0:T(8,128)S(1)}, f32[1,16,128]{2,1,0:T(8,128)S(1)}, u32[]{:S(2)}, u32[]{:S(2)}) collective-permute-start(f32[1,16,128]{2,1,0:T(8,128)S(1)} %get-tuple-element.775), channel_id=1, source_target_pairs={{0,16},{16,32},{32,48},{48,64},{64,80},{80,96},{96,112},{112,128},... | collective-permute-start | bytes 24584 | tf_op jit(solution)/shard_map/while/body/eval_jaxpr/ppermute | solution.py:23
  73.6 18.0 %collective-permute-start.12 = (f32[1,8,64]{2,1,0:T(8,128)S(1)}, f32[1,8,64]{2,1,0:T(8,128)S(1)}, u32[]{:S(2)}, u32[]{:S(2)}) collective-permute-start(f32[1,8,64]{2,1,0:T(8,128)S(1)} %get-tuple-element.814), channel_id=1, source_target_pairs={{16,0},{32,16},{48,32},{64,48},{80,64},{96,80},{112,96},{128,112},... | collective-permute-start | bytes 6152 | tf_op jit(solution)/shard_map/while/body/eval_jaxpr/ppermute | solution.py:24
  83.1 8.6 %collective-permute-start.13 = (f32[1,8,64]{2,1,0:T(8,128)S(1)}, f32[1,8,64]{2,1,0:T(8,128)S(1)}, u32[]{:S(2)}, u32[]{:S(2)}) collective-permute-start(f32[1,8,64]{2,1,0:T(8,128)S(1)} %get-tuple-element.815), channel_id=1, source_target_pairs={{0,16},{16,32},{32,48},{48,64},{64,80},{80,96},{96,112},{112,128},... | collective-permute-start | bytes 6152 | tf_op jit(solution)/shard_map/while/body/eval_jaxpr/ppermute | solution.py:23
  86.1 85.8 %collective-permute-start.38 = (f32[4,1,16]{2,1,0:T(1,128)S(1)}, f32[4,1,16]{2,1,0:T(1,128)S(1)}, u32[]{:S(2)}, u32[]{:S(2)}) collective-permute-start(f32[4,1,16]{2,1,0:T(1,128)S(1)} %get-tuple-element.892), channel_id=1, source_target_pairs={{0,1},{1,2},{2,3},{3,4},{4,5},{5,6},{6,7},{7,8},{8,9},{9,10},{10,1... | collective-permute-start | bytes 776 | tf_op jit(solution)/shard_map/while/body/eval_jaxpr/ppermute | solution.py:23
  86.1 85.8 %collective-permute-start.39 = (f32[4,1,16]{2,1,0:T(1,128)S(1)}, f32[4,1,16]{2,1,0:T(1,128)S(1)}, u32[]{:S(2)}, u32[]{:S(2)}) collective-permute-start(f32[4,1,16]{2,1,0:T(1,128)S(1)} %get-tuple-element.893), channel_id=1, source_target_pairs={{1,0},{2,1},{3,2},{4,3},{5,4},{6,5},{7,6},{8,7},{9,8},{10,9},{11,1... | collective-permute-start | bytes 776 | tf_op jit(solution)/shard_map/while/body/eval_jaxpr/ppermute | solution.py:24
  91.5 53.0 %collective-permute-start.26 = (f32[6,1,32]{2,1,0:T(1,128)S(1)}, f32[6,1,32]{2,1,0:T(1,128)S(1)}, u32[]{:S(2)}, u32[]{:S(2)}) collective-permute-start(f32[6,1,32]{2,1,0:T(1,128)S(1)} %get-tuple-element.854), channel_id=1, source_target_pairs={{1,0},{2,1},{3,2},{4,3},{5,4},{6,5},{7,6},{8,7},{9,8},{10,9},{11,1... | collective-permute-start | bytes 2312 | tf_op jit(solution)/shard_map/while/body/eval_jaxpr/ppermute | solution.py:24
  91.7 7.1 collective-permute-start.3
  110.1 7.1 collective-permute-start.7
  122.7 7.1 collective-permute-start.11
  126.3 18.6 %collective-permute-start.27 = (f32[6,1,32]{2,1,0:T(1,128)S(1)}, f32[6,1,32]{2,1,0:T(1,128)S(1)}, u32[]{:S(2)}, u32[]{:S(2)}) collective-permute-start(f32[6,1,32]{2,1,0:T(1,128)S(1)} %get-tuple-element.855), channel_id=1, source_target_pairs={{0,1},{1,2},{2,3},{3,4},{4,5},{5,6},{6,7},{7,8},{8,9},{9,10},{10,1... | collective-permute-start | bytes 2312 | tf_op jit(solution)/shard_map/while/body/eval_jaxpr/ppermute | solution.py:23
  162.6 7.0 collective-permute-start.23
  187.4 7.2 collective-permute-start.35
  259.0 7.0 collective-permute-start.63
  294.0 7.1 collective-permute-start.71
  306.3 7.1 collective-permute-start.75
  314.5 26.8 %collective-permute-start = (f32[1,16,128]{2,1,0:T(8,128)S(1)}, f32[1,16,128]{2,1,0:T(8,128)S(1)}, u32[]{:S(2)}, u32[]{:S(2)}) collective-permute-start(f32[1,16,128]{2,1,0:T(8,128)S(1)} %get-tuple-element.774), channel_id=1, source_target_pairs={{16,0},{32,16},{48,32},{64,48},{80,64},{96,80},{112,96},{128,112},... | collective-permute-start | bytes 24584 | tf_op jit(solution)/shard_map/while/body/eval_jaxpr/ppermute | solution.py:24
  314.5 32.2 %collective-permute-start.1 = (f32[1,16,128]{2,1,0:T(8,128)S(1)}, f32[1,16,128]{2,1,0:T(8,128)S(1)}, u32[]{:S(2)}, u32[]{:S(2)}) collective-permute-start(f32[1,16,128]{2,1,0:T(8,128)S(1)} %get-tuple-element.775), channel_id=1, source_target_pairs={{0,16},{16,32},{32,48},{48,64},{64,80},{80,96},{96,112},{112,128},... | collective-permute-start | bytes 24584 | tf_op jit(solution)/shard_map/while/body/eval_jaxpr/ppermute | solution.py:23
  328.8 18.0 %collective-permute-start.12 = (f32[1,8,64]{2,1,0:T(8,128)S(1)}, f32[1,8,64]{2,1,0:T(8,128)S(1)}, u32[]{:S(2)}, u32[]{:S(2)}) collective-permute-start(f32[1,8,64]{2,1,0:T(8,128)S(1)} %get-tuple-element.814), channel_id=1, source_target_pairs={{16,0},{32,16},{48,32},{64,48},{80,64},{96,80},{112,96},{128,112},... | collective-permute-start | bytes 6152 | tf_op jit(solution)/shard_map/while/body/eval_jaxpr/ppermute | solution.py:24
  338.3 8.6 %collective-permute-start.13 = (f32[1,8,64]{2,1,0:T(8,128)S(1)}, f32[1,8,64]{2,1,0:T(8,128)S(1)}, u32[]{:S(2)}, u32[]{:S(2)}) collective-permute-start(f32[1,8,64]{2,1,0:T(8,128)S(1)} %get-tuple-element.815), channel_id=1, source_target_pairs={{0,16},{16,32},{32,48},{48,64},{64,80},{80,96},{96,112},{112,128},... | collective-permute-start | bytes 6152 | tf_op jit(solution)/shard_map/while/body/eval_jaxpr/ppermute | solution.py:23
  341.3 86.0 %collective-permute-start.38 = (f32[4,1,16]{2,1,0:T(1,128)S(1)}, f32[4,1,16]{2,1,0:T(1,128)S(1)}, u32[]{:S(2)}, u32[]{:S(2)}) collective-permute-start(f32[4,1,16]{2,1,0:T(1,128)S(1)} %get-tuple-element.892), channel_id=1, source_target_pairs={{0,1},{1,2},{2,3},{3,4},{4,5},{5,6},{6,7},{7,8},{8,9},{9,10},{10,1... | collective-permute-start | bytes 776 | tf_op jit(solution)/shard_map/while/body/eval_jaxpr/ppermute | solution.py:23
  341.3 86.0 %collective-permute-start.39 = (f32[4,1,16]{2,1,0:T(1,128)S(1)}, f32[4,1,16]{2,1,0:T(1,128)S(1)}, u32[]{:S(2)}, u32[]{:S(2)}) collective-permute-start(f32[4,1,16]{2,1,0:T(1,128)S(1)} %get-tuple-element.893), channel_id=1, source_target_pairs={{1,0},{2,1},{3,2},{4,3},{5,4},{6,5},{7,6},{8,7},{9,8},{10,9},{11,1... | collective-permute-start | bytes 776 | tf_op jit(solution)/shard_map/while/body/eval_jaxpr/ppermute | solution.py:24
  346.7 53.2 %collective-permute-start.26 = (f32[6,1,32]{2,1,0:T(1,128)S(1)}, f32[6,1,32]{2,1,0:T(1,128)S(1)}, u32[]{:S(2)}, u32[]{:S(2)}) collective-permute-start(f32[6,1,32]{2,1,0:T(1,128)S(1)} %get-tuple-element.854), channel_id=1, source_target_pairs={{1,0},{2,1},{3,2},{4,3},{5,4},{6,5},{7,6},{8,7},{9,8},{10,9},{11,1... | collective-permute-start | bytes 2312 | tf_op jit(solution)/shard_map/while/body/eval_jaxpr/ppermute | solution.py:24
  346.9 7.1 collective-permute-start.3
  365.3 7.1 collective-permute-start.7
  378.1 7.1 collective-permute-start.11
  381.8 18.6 %collective-permute-start.27 = (f32[6,1,32]{2,1,0:T(1,128)S(1)}, f32[6,1,32]{2,1,0:T(1,128)S(1)}, u32[]{:S(2)}, u32[]{:S(2)}) collective-permute-start(f32[6,1,32]{2,1,0:T(1,128)S(1)} %get-tuple-element.855), channel_id=1, source_target_pairs={{0,1},{1,2},{2,3},{3,4},{4,5},{5,6},{6,7},{7,8},{8,9},{9,10},{10,1... | collective-permute-start | bytes 2312 | tf_op jit(solution)/shard_map/while/body/eval_jaxpr/ppermute | solution.py:23
  418.0 7.0 collective-permute-start.23
  442.8 7.2 collective-permute-start.35
  526.4 7.0 collective-permute-start.67
  549.2 7.1 collective-permute-start.71
  561.5 7.1 collective-permute-start.75
  569.9 26.8 %collective-permute-start = (f32[1,16,128]{2,1,0:T(8,128)S(1)}, f32[1,16,128]{2,1,0:T(8,128)S(1)}, u32[]{:S(2)}, u32[]{:S(2)}) collective-permute-start(f32[1,16,128]{2,1,0:T(8,128)S(1)} %get-tuple-element.774), channel_id=1, source_target_pairs={{16,0},{32,16},{48,32},{64,48},{80,64},{96,80},{112,96},{128,112},... | collective-permute-start | bytes 24584 | tf_op jit(solution)/shard_map/while/body/eval_jaxpr/ppermute | solution.py:24
  570.0 32.2 %collective-permute-start.1 = (f32[1,16,128]{2,1,0:T(8,128)S(1)}, f32[1,16,128]{2,1,0:T(8,128)S(1)}, u32[]{:S(2)}, u32[]{:S(2)}) collective-permute-start(f32[1,16,128]{2,1,0:T(8,128)S(1)} %get-tuple-element.775), channel_id=1, source_target_pairs={{0,16},{16,32},{32,48},{48,64},{64,80},{80,96},{96,112},{112,128},... | collective-permute-start | bytes 24584 | tf_op jit(solution)/shard_map/while/body/eval_jaxpr/ppermute | solution.py:23
  584.2 18.0 %collective-permute-start.12 = (f32[1,8,64]{2,1,0:T(8,128)S(1)}, f32[1,8,64]{2,1,0:T(8,128)S(1)}, u32[]{:S(2)}, u32[]{:S(2)}) collective-permute-start(f32[1,8,64]{2,1,0:T(8,128)S(1)} %get-tuple-element.814), channel_id=1, source_target_pairs={{16,0},{32,16},{48,32},{64,48},{80,64},{96,80},{112,96},{128,112},... | collective-permute-start | bytes 6152 | tf_op jit(solution)/shard_map/while/body/eval_jaxpr/ppermute | solution.py:24
  593.8 8.6 %collective-permute-start.13 = (f32[1,8,64]{2,1,0:T(8,128)S(1)}, f32[1,8,64]{2,1,0:T(8,128)S(1)}, u32[]{:S(2)}, u32[]{:S(2)}) collective-permute-start(f32[1,8,64]{2,1,0:T(8,128)S(1)} %get-tuple-element.815), channel_id=1, source_target_pairs={{0,16},{16,32},{32,48},{48,64},{64,80},{80,96},{96,112},{112,128},... | collective-permute-start | bytes 6152 | tf_op jit(solution)/shard_map/while/body/eval_jaxpr/ppermute | solution.py:23
  596.7 85.8 %collective-permute-start.38 = (f32[4,1,16]{2,1,0:T(1,128)S(1)}, f32[4,1,16]{2,1,0:T(1,128)S(1)}, u32[]{:S(2)}, u32[]{:S(2)}) collective-permute-start(f32[4,1,16]{2,1,0:T(1,128)S(1)} %get-tuple-element.892), channel_id=1, source_target_pairs={{0,1},{1,2},{2,3},{3,4},{4,5},{5,6},{6,7},{7,8},{8,9},{9,10},{10,1... | collective-permute-start | bytes 776 | tf_op jit(solution)/shard_map/while/body/eval_jaxpr/ppermute | solution.py:23
  596.7 85.8 %collective-permute-start.39 = (f32[4,1,16]{2,1,0:T(1,128)S(1)}, f32[4,1,16]{2,1,0:T(1,128)S(1)}, u32[]{:S(2)}, u32[]{:S(2)}) collective-permute-start(f32[4,1,16]{2,1,0:T(1,128)S(1)} %get-tuple-element.893), channel_id=1, source_target_pairs={{1,0},{2,1},{3,2},{4,3},{5,4},{6,5},{7,6},{8,7},{9,8},{10,9},{11,1... | collective-permute-start | bytes 776 | tf_op jit(solution)/shard_map/while/body/eval_jaxpr/ppermute | solution.py:24
  602.1 53.0 %collective-permute-start.26 = (f32[6,1,32]{2,1,0:T(1,128)S(1)}, f32[6,1,32]{2,1,0:T(1,128)S(1)}, u32[]{:S(2)}, u32[]{:S(2)}) collective-permute-start(f32[6,1,32]{2,1,0:T(1,128)S(1)} %get-tuple-element.854), channel_id=1, source_target_pairs={{1,0},{2,1},{3,2},{4,3},{5,4},{6,5},{7,6},{8,7},{9,8},{10,9},{11,1... | collective-permute-start | bytes 2312 | tf_op jit(solution)/shard_map/while/body/eval_jaxpr/ppermute | solution.py:24
  602.4 7.1 collective-permute-start.3
  620.8 7.1 collective-permute-start.7
  633.3 7.1 collective-permute-start.11
  637.0 18.6 %collective-permute-start.27 = (f32[6,1,32]{2,1,0:T(1,128)S(1)}, f32[6,1,32]{2,1,0:T(1,128)S(1)}, u32[]{:S(2)}, u32[]{:S(2)}) collective-permute-start(f32[6,1,32]{2,1,0:T(1,128)S(1)} %get-tuple-element.855), channel_id=1, source_target_pairs={{0,1},{1,2},{2,3},{3,4},{4,5},{5,6},{6,7},{7,8},{8,9},{9,10},{10,1... | collective-permute-start | bytes 2312 | tf_op jit(solution)/shard_map/while/body/eval_jaxpr/ppermute | solution.py:23
  698.0 7.2 collective-permute-start.35
  769.6 7.0 collective-permute-start.63
  781.8 7.0 collective-permute-start.67
  804.6 7.1 collective-permute-start.71
  817.0 7.1 collective-permute-start.75
  (181 other events, 689.4 us)
